TPU v7x, 32 devices: a whole 2x2x4 slice. The times are simulated.
32 devices in a mesh: group: 2 (over y), expert: 4 (over z), tensor: 2 (over x), seq: 2 (over core).
Axes of the slice: x: 2, y: 2, z: 4, core: 2. Of those that a mesh axis runs over, the one named last changes fastest.
Arguments:
- queries: bfloat16 [2048, 2048], P(('group', 'expert', 'seq'), 'tensor'), parts along dimension 0, may hold values from -6 to 6
- keys_values: bfloat16 [2048, 4, 128], P(('group', 'expert', 'seq'), 'tensor'), parts along dimension 0, may hold values from -6 to 6
- residual: bfloat16 [2048, 1440], P(('group', 'expert', 'seq')), parts along dimension 0, may hold values from -6 to 6
- sink_logits: float32 [32], P('tensor'), may hold values from 0 to 6
- norm_gain: float32 [1440], replicated, may hold values from 0.5 to 1.5
- out_proj: bfloat16 [2048, 1440], P('tensor', 'seq'), may hold values from -0.125 to 0.125
- shared_gate_up: bfloat16 [1440, 2, 512], P('seq', None, 'tensor'), may hold values from -0.15625 to 0.15625
- shared_down: bfloat16 [512, 1440], P('tensor', 'seq'), may hold values from -0.25 to 0.25
- expert_gate_up: bfloat16 [8, 1440, 2, 1440], P(('expert', 'seq'), None, None, 'tensor'), may hold values from -0.15625 to 0.15625
- expert_down: bfloat16 [8, 1440, 1440], P(('expert', 'seq'), 'tensor'), may hold values from -0.15625 to 0.15625
- expert_ids: int32 [2048, 4], P(('group', 'expert', 'seq')), parts along dimension 0, may hold values from 0 to 7, all different within a row; in each aligned block of 128 rows (0 to 127, 128 to 255, ...) at most 96 rows name the same one
- gate_weights: float32 [2048, 4], P(('group', 'expert', 'seq')), parts along dimension 0, may hold values from 0.1 to 1
Outputs:
- mixed: bfloat16 [2048, 1440], P(('group', 'expert', 'seq'), 'tensor'), parts along dimension 0
There are 2 independent parts, one for each index of `group`. A program takes and returns all parts, laid end to end along the dimension named above; an argument that names none is the same for every part. Nothing has to cross between parts.
Inputs may be any that keep to these rules, and one draw needn't show every extreme that they name: `expert_ids`: in each aligned block of 128 tokens (the tokens of one device), no expert is named by more than 96 tokens; the 4 ids of a token differ.
All inputs are finite; a program needn't handle non-finite values.
Results may differ from a plain program's by a relative error of at most 0.014.
Values may be sent and summed in bfloat16 or wider, within the bound.
A program may use at most 64 MiB of HBM per device.

v0:
```python
import math

import jax
import jax.numpy as jnp
from jax import lax
from jax.sharding import PartitionSpec as P

WINDOW = 128


norm_eps = 1e-05
glu_alpha = 1.702


def shifted(value, axis, steps):
    count = lax.axis_size(axis)
    initial, last = (max(0, -steps), min(count, count - steps))
    return lax.ppermute(value, axis, [(source, source + steps) for source in range(initial, last)])


def glu_act(gate_pre, up_pre):
    return (up_pre + 1.0) * gate_pre * jax.nn.sigmoid(glu_alpha * gate_pre)


def attend_local(queries, keys_values, sink_logits, block_index):
    count_rows = queries.shape[0]
    kv_count = keys_values.shape[1]
    head_size = keys_values.shape[2] // 2
    group_size = queries.shape[1] // (head_size * kv_count)
    earlier = shifted(keys_values, ("expert", "seq"), 1)
    pair_block = jnp.concatenate([earlier, keys_values], axis=0)
    grouped = queries.reshape(count_rows, kv_count, group_size, head_size)
    key_part = pair_block[:, :, :head_size]
    value_part = pair_block[:, :, head_size:]
    scores = jnp.einsum(
        "pkgd,jkd->kgpj", grouped, key_part, preferred_element_type=jnp.float32
    ) / math.sqrt(head_size)
    query_pos = jnp.arange(count_rows, dtype=jnp.int32)[:, None]
    key_rel = jnp.arange(2 * count_rows, dtype=jnp.int32)[None, :] - count_rows
    distance = query_pos - key_rel
    visible = (distance >= 0) & (distance < WINDOW) & (block_index * count_rows + key_rel >= 0)
    scores = jnp.where(visible[None, None], scores, -jnp.inf)
    sink_term = sink_logits.reshape(kv_count, group_size)[:, :, None, None]
    top_score = jnp.maximum(jnp.max(scores, axis=-1, keepdims=True), sink_term)
    expo = jnp.exp(scores - top_score)
    denom = jnp.sum(expo, axis=-1, keepdims=True) + jnp.exp(sink_term - top_score)
    attn_weights = (expo / denom).astype(jnp.bfloat16)
    context = jnp.einsum(
        "kgpj,jkd->pkgd", attn_weights, value_part, preferred_element_type=jnp.float32
    )
    return context.astype(jnp.bfloat16).reshape(count_rows, kv_count * group_size * head_size)


def local(
    queries,
    keys_values,
    residual,
    sink_logits,
    norm_gain,
    out_proj,
    shared_gate_up,
    shared_down,
    expert_gate_up,
    expert_down,
    expert_ids,
    gate_weights,
):
    block_index = lax.axis_index(("expert", "seq"))
    context = attend_local(queries, keys_values, sink_logits, block_index)
    proj_full, shared_gu_full, shared_dn_full = (
        lax.all_gather(out_proj, "seq", axis=1, tiled=True),
        lax.all_gather(shared_gate_up, "seq", axis=0, tiled=True),
        lax.all_gather(shared_down, "seq", axis=1, tiled=True),
    )
    attn_part = jnp.dot(context, proj_full, preferred_element_type=jnp.float32)
    attn = lax.psum(attn_part.astype(jnp.bfloat16), "tensor").astype(jnp.float32)
    stream = residual.astype(jnp.float32) + attn
    scale = lax.rsqrt(jnp.mean(stream * stream, axis=-1, keepdims=True) + norm_eps)
    normed = (stream * scale * norm_gain).astype(jnp.bfloat16)
    shared_pre = jnp.einsum(
        "pd,dcf->pcf", normed, shared_gu_full, preferred_element_type=jnp.float32
    )
    shared_hidden = glu_act(shared_pre[:, 0], shared_pre[:, 1]).astype(jnp.bfloat16)
    shared_part = jnp.dot(shared_hidden, shared_dn_full, preferred_element_type=jnp.float32)
    count_rows = normed.shape[0]
    width = normed.shape[1]
    top_count = expert_ids.shape[1]
    expert_count = expert_gate_up.shape[0] * lax.axis_size(("expert", "seq"))
    capacity = max(2, 3 * count_rows * top_count // (2 * expert_count))
    tensor_size = lax.axis_size("tensor")
    col_width = width // tensor_size
    col_start = lax.axis_index("tensor") * col_width
    flat_ids = expert_ids.reshape(-1)
    assign_count = count_rows * top_count
    onehot = (flat_ids[:, None] == jnp.arange(expert_count, dtype=jnp.int32)[None, :]).astype(
        jnp.int32
    )
    ranks = jnp.sum((jnp.cumsum(onehot, axis=0) - 1) * onehot, axis=1)
    slots = flat_ids * capacity + ranks
    slot_source = (
        jnp.full((expert_count * capacity,), assign_count, jnp.int32)
        .at[slots]
        .set(jnp.arange(assign_count, dtype=jnp.int32))
    )
    token_of_slot = jnp.where(slot_source < assign_count, slot_source // top_count, count_rows)
    normed_padded = jnp.concatenate([normed, jnp.zeros((1, width), jnp.bfloat16)], axis=0)
    outgoing = normed_padded[token_of_slot].reshape(expert_count, capacity, width)
    arrived = lax.all_to_all(outgoing, ("expert", "seq"), split_axis=0, concat_axis=0, tiled=True)
    expert_pre = jnp.einsum(
        "scd,dhf->schf", arrived, expert_gate_up[0], preferred_element_type=jnp.float32
    )
    expert_hidden = glu_act(expert_pre[:, :, 0], expert_pre[:, :, 1]).astype(jnp.bfloat16)
    expert_part = jnp.einsum(
        "scf,fd->scd", expert_hidden, expert_down[0], preferred_element_type=jnp.float32
    )
    returned = lax.all_to_all(
        expert_part.astype(jnp.bfloat16), ("expert", "seq"), split_axis=0, concat_axis=0, tiled=True
    )
    picked = (
        returned.reshape(expert_count * capacity, width)[slots]
        .astype(jnp.float32)
        .reshape(count_rows, top_count, width)
    )
    routed = jnp.sum(picked * gate_weights[:, :, None], axis=1)
    shared_rounded = lax.optimization_barrier(shared_part.astype(jnp.bfloat16))
    combined = shared_rounded.astype(jnp.float32) + routed
    summed = lax.psum_scatter(
        combined.astype(jnp.bfloat16), "tensor", scatter_dimension=1, tiled=True
    ).astype(jnp.float32)
    stream_cols = lax.dynamic_slice_in_dim(stream, col_start, col_width, 1)
    return (stream_cols + summed).astype(jnp.bfloat16)


def solution(mesh):
    in_specs = (
        P(("group", "expert", "seq"), "tensor"),
        P(("group", "expert", "seq"), "tensor", None),
        P(("group", "expert", "seq"), None),
        P("tensor"),
        P(),
        P("tensor", "seq"),
        P("seq", None, "tensor"),
        P("tensor", "seq"),
        P(("expert", "seq"), None, None, "tensor"),
        P(("expert", "seq"), "tensor", None),
        P(("group", "expert", "seq"), None),
        P(("group", "expert", "seq"), None),
    )
    out_specs = P(("group", "expert", "seq"), "tensor")
    return jax.shard_map(local, mesh=mesh, in_specs=in_specs, out_specs=out_specs, check_vma=False)
```

profile of v0, /device:TPU:0, one launch (start us, length us, event | category | flops | bytes accessed | tf_op | source)
XLA Modules:
  0.0 226.2 jit_solution(841056464610995412)
XLA Ops:
  6.5 0.0 copy-start
  6.5 0.0 copy-start.5
  6.5 0.0 all-gather.3.cloned.1.call-start
  6.5 0.7 all-gather.3.cloned.1.call-update
  7.3 0.0 all-reduce.3.cloned.1.call-start
  7.3 1.0 copy.32
  8.3 2.4 %collective-permute-start = (bf16[128,2,128]{0,2,1:T(8,128)(2,1)S(1)}, bf16[128,2,128]{0,2,1:T(8,128)(2,1)S(1)}, u32[]{:S(2)}, u32[]{:S(2)}) collective-permute-start(bf16[128,2,128]{0,2,1:T(8,128)(2,1)S(1)} %copy.32), channel_id=1, source_target_pairs={{0,1},{1,4},{4,5},{5,8},{8,9},{9,12},{12,13},{2,3},{3,6},{6,7},{7,... | collective-permute-start | bytes 196616 | tf_op jit(solution)/shard_map/ppermute | solution.py:18
  10.7 0.8 copy.38
  11.5 0.1 eq.29
  11.6 0.1 eq.25
  11.7 1.1 copy.34
  12.8 0.7 max.18
  13.6 1.1 reduce-window.6
  14.7 0.2 slice_reduce_fusion
  15.0 0.0 copy-done.5
  15.0 0.1 copy.37
  15.1 0.1 mul.101
  15.2 0.1 fusion.20
  15.4 0.1 fusion.30
  15.4 0.0 collective-permute-done
  15.5 0.5 fusion.43
  15.9 0.1 broadcast_maximum_fusion
  16.0 0.3 fusion.8
  16.3 0.1 exponential_add_fusion
  16.4 0.5 convolution_convert_fusion.3
  16.9 6.6 %all-gather.3.cloned.1.call-done = bf16[1024,1440]{0,1:T(8,128)(2,1)} async-done(((bf16[1024,720]{0,1:T(8,128)(2,1)}), bf16[1024,1440]{0,1:T(8,128)(2,1)}) %all-gather.3.cloned.1.call-update) | async-done | bytes 2949136 | tf_op jit(solution)/shard_map/all_gather | solution.py:71
  23.5 0.0 copy-start.1
  23.5 0.0 copy-start.4
  23.5 3.6 %convolution_convert_fusion.1 = bf16[128,1440]{0,1:T(8,128)(2,1)} fusion(bf16[1024,1440]{0,1:T(8,128)(2,1)} %all-gather.3.cloned.1.call-done, bf16[128,1024]{0,1:T(8,128)(2,1)S(1)} %bitcast.61), kind=kOutput, calls=%fused_computation.8 | convolution fusion | flops 377671680 | bytes 3579904 | tf_op jit(solution)/shard_map/dot_general | solution.py:75
  27.0 0.0 all-reduce.3.cloned.1.call-update
  27.1 2.4 %scatter_custom_fusion = s32[768]{0:T(1024)S(1)} fusion(s32[512]{0:T(512)S(1)} %bitcast.57, s32[512]{0:T(512)S(1)} %iota.27, s32[]{:T(128)} %constant.70.clone.1), kind=kCustom, calls=%fused_computation.68 | custom fusion | bytes 3076 | tf_op jit(solution)/shard_map/scatter | solution.py:103
  29.6 24.1 %all-reduce.3.cloned.1.call-done = bf16[128,1440]{0,1:T(8,128)(2,1)} async-done(((bf16[128,1440]{0,1:T(8,128)(2,1)}), bf16[128,1440]{0,1:T(8,128)(2,1)}) %all-reduce.3.cloned.1.call-update) | async-done | bytes 368656 | tf_op jit(solution)/shard_map/psum | solution.py:76
  53.6 0.0 copy-done.1
  53.6 2.0 convert_add_fusion
  55.6 0.0 copy-done.4
  55.6 1.2 multiply_convert_fusion
  56.9 0.2 copy.48
  57.1 3.8 %gather_fusion = bf16[768,1440]{1,0:T(8,128)(2,1)} fusion(bf16[129,1440]{1,0:T(8,128)(2,1)S(1)} %concatenate.7.clone, s32[1024]{0:T(1024)S(1)} %pad_clamp_fusion.1), kind=kCustom, calls=%fused_computation | custom fusion | bytes 4426752 | tf_op jit(solution)/shard_map/gather | solution.py:107
  60.9 59.3 %all_to_all.10 = bf16[8,96,1440]{2,1,0:T(8,128)(2,1)S(1)} all-to-all(bf16[8,96,1440]{2,1,0:T(8,128)(2,1)} %bitcast.55), channel_id=1, replica_groups=mesh['group'=2,'expert'=4,'tensor'=2,'seq'=2] {'expert','seq'}, dimensions={0} | all-to-all | bytes 4423680 | tf_op jit(solution)/shard_map/all_to_all | solution.py:108
  120.2 6.0 %fusion = f32[8,96,2,720]{3,1,2,0:T(8,128)S(1)} fusion(bf16[1440,2,720]{2,1,0:T(2,128)(2,1)} %bitcast.60, bf16[8,96,1440]{2,1,0:T(8,128)(2,1)S(1)} %all_to_all.10), kind=kOutput, calls=%fused_computation.3 | convolution fusion | flops 3185049600 | bytes 10782720 | tf_op jit(solution)/shard_map/scd,dhf->schf/dot_general | solution.py:109
  126.2 0.0 copy-done
  126.2 3.5 %convolution_convert_fusion = bf16[8,96,1440]{2,1,0:T(8,128)(2,1)} fusion(bf16[1,720,1440]{2,1,0:T(8,128)(2,1)S(1)} %copy-done, f32[8,96,2,720]{3,1,2,0:T(8,128)S(1)} %fusion), kind=kOutput, calls=%fused_computation.6 | convolution fusion | flops 1598054400 | bytes 8709120 | tf_op jit(solution)/shard_map/scf,fd->scd/dot_general | solution.py:113
  129.7 4.5 %all-to-all-start.1 = ((bf16[8,96,1440]{2,1,0:T(8,128)(2,1)}), bf16[8,96,1440]{2,1,0:T(8,128)(2,1)}, u32[]{:S(2)}, u32[]{:S(2)}) async-start(bf16[8,96,1440]{2,1,0:T(8,128)(2,1)} %convolution_convert_fusion), calls=%async_computation.1 | async-start | bytes 4718592 | tf_op jit(solution)/shard_map/all_to_all | solution.py:116
  134.2 0.0 all-gather.5.cloned.1.call-start
  134.2 0.0 copy-done.2
  134.3 1.0 copy.36
  135.2 0.0 all-gather.5.cloned.1.call-update
  135.2 0.0 reduce-scatter.2.cloned.1.call-start
  135.3 0.0 copy-done.6
  135.3 0.1 copy.42
  135.4 2.7 %all_gather.11 = bf16[256,1440]{0,1:T(8,128)(2,1)S(1)} all-gather(bf16[256,720]{0,1:T(8,128)(2,1)} %param.19), channel_id=1, replica_groups=mesh['group'=2,'expert'=4,'tensor'=2,'seq'=2] {'seq'}, dimensions={1}, use_global_device_ids=true | all-gather | bytes 1105920 | tf_op jit(solution)/shard_map/all_gather | solution.py:73
  138.1 8.6 %all-gather.5.cloned.1.call-done = bf16[1440,2,256]{2,0,1:T(8,128)(2,1)} async-done(((bf16[720,2,256]{2,0,1:T(8,128)(2,1)}), bf16[1440,2,256]{2,0,1:T(8,128)(2,1)}) %all-gather.5.cloned.1.call-update) | async-done | bytes 1474576 | tf_op jit(solution)/shard_map/all_gather | solution.py:72
  146.8 1.8 fusion.12
  148.6 1.1 convolution_convert_fusion.2
  149.7 39.1 %all-to-all-done.1 = bf16[8,96,1440]{2,1,0:T(8,128)(2,1)} async-done(((bf16[8,96,1440]{2,1,0:T(8,128)(2,1)}), bf16[8,96,1440]{2,1,0:T(8,128)(2,1)}, u32[]{:S(2)}, u32[]{:S(2)}) %all-to-all-start.1) | async-done | bytes 2211872 | tf_op jit(solution)/shard_map/all_to_all | solution.py:116
  188.8 6.4 %gather_fusion.1 = bf16[512,1440]{1,0:T(8,128)(2,1)} fusion(bf16[768,1440]{1,0:T(8,128)(2,1)} %bitcast.22, s32[1024]{0:T(1024)S(1)} %pad_clamp_fusion), kind=kCustom, calls=%fused_computation.1 | custom fusion | bytes 2951168 | tf_op jit(solution)/shard_map/gather | solution.py:120
  195.2 4.2 %reshape.154 = f32[128,4,1440]{2,1,0:T(4,128)} reshape(bf16[512,1440]{1,0:T(8,128)(2,1)} %gather_fusion.1) | data formatting | bytes 4423680 | tf_op jit(solution)/shard_map/convert_element_type | solution.py:121
  199.4 4.2 %multiply_reduce_fusion = f32[128,1440]{1,0:T(8,128)S(1)} fusion(f32[128,4,1440]{2,1,0:T(4,128)} %reshape.154, f32[128,4]{1,0:T(8,128)S(1)} %copy.42), kind=kLoop, calls=%fused_computation.7 | loop fusion | flops 1290240 | bytes 3688448 | tf_op jit(solution)/shard_map/reduce_sum | solution.py:124
  203.6 1.1 copy.43
  204.8 0.0 copy-done.3
  204.8 1.9 add_convert_fusion
  206.7 0.0 reduce-scatter.2.cloned.1.call-update
  206.7 11.2 %reduce-scatter.2.cloned.1.call-done = bf16[128,720]{0,1:T(8,128)(2,1)} async-done(((bf16[128,1440]{0,1:T(8,128)(2,1)}), bf16[128,720]{0,1:T(8,128)(2,1)}) %reduce-scatter.2.cloned.1.call-update) | async-done | bytes 184336 | tf_op jit(solution)/shard_map/reduce_scatter | solution.py:127
  217.9 1.8 add_convert_fusion.1
  (16 shorter events, 0.1 us)
Async XLA Ops:
  6.5 119.7 %copy-start = (bf16[1,720,1440]{2,1,0:T(8,128)(2,1)S(1)}, bf16[1,720,1440]{2,1,0:T(8,128)(2,1)}, u32[]{:S(2)}) copy-start(bf16[1,720,1440]{2,1,0:T(8,128)(2,1)} %param.21) | copy-start | bytes 6220804
  6.5 8.4 %copy-start.5 = (s32[128,4]{0,1:T(4,128)S(1)}, s32[128,4]{0,1:T(4,128)}, u32[]{:S(2)}) copy-start(s32[128,4]{0,1:T(4,128)} %param.22) | copy-start | bytes 6148
  6.5 16.9 %all-gather.3.cloned.1.call-start = ((), (), s32[]{:S(2)}) async-start(), calls=%async_computation.3 | async-start | bytes 4423680 | tf_op jit(solution)/shard_map/all_gather | solution.py:71
  7.3 46.4 %all-reduce.3.cloned.1.call-start = ((), (), s32[]{:S(2)}) async-start(), calls=%async_computation.4 | async-start | bytes 737280 | tf_op jit(solution)/shard_map/psum | solution.py:76
  8.3 7.2 %collective-permute-start = (bf16[128,2,128]{0,2,1:T(8,128)(2,1)S(1)}, bf16[128,2,128]{0,2,1:T(8,128)(2,1)S(1)}, u32[]{:S(2)}, u32[]{:S(2)}) collective-permute-start(bf16[128,2,128]{0,2,1:T(8,128)(2,1)S(1)} %copy.32), channel_id=1, source_target_pairs={{0,1},{1,4},{4,5},{5,8},{8,9},{9,12},{12,13},{2,3},{3,6},{6,7},{7,... | collective-permute-start | bytes 196616 | tf_op jit(solution)/shard_map/ppermute | solution.py:18
  23.5 30.2 %copy-start.1 = (bf16[128,1440]{0,1:T(8,128)(2,1)S(1)}, bf16[128,1440]{0,1:T(8,128)(2,1)}, u32[]{:S(2)}) copy-start(bf16[128,1440]{0,1:T(8,128)(2,1)} %param.14) | copy-start | bytes 1105924
  23.5 32.2 %copy-start.4 = (f32[1440]{0:T(1024)S(1)}, f32[1440]{0:T(1024)}, u32[]{:S(2)}) copy-start(f32[1440]{0:T(1024)} %param.16) | copy-start | bytes 17284
  129.7 4.6 %copy-start.2 = (bf16[720,2,256]{2,1,0:T(2,128)(2,1)S(1)}, bf16[720,2,256]{2,1,0:T(2,128)(2,1)}, u32[]{:S(2)}) copy-start(bf16[720,2,256]{2,1,0:T(2,128)(2,1)} %param.18) | copy-start | bytes 2211844
  129.7 5.6 %copy-start.6 = (f32[128,4]{0,1:T(4,128)S(1)}, f32[128,4]{0,1:T(4,128)}, u32[]{:S(2)}) copy-start(f32[128,4]{0,1:T(4,128)} %param.23) | copy-start | bytes 6148
  129.7 59.2 %all-to-all-start.1 = ((bf16[8,96,1440]{2,1,0:T(8,128)(2,1)}), bf16[8,96,1440]{2,1,0:T(8,128)(2,1)}, u32[]{:S(2)}, u32[]{:S(2)}) async-start(bf16[8,96,1440]{2,1,0:T(8,128)(2,1)} %convolution_convert_fusion), calls=%async_computation.1 | async-start | bytes 4718592 | tf_op jit(solution)/shard_map/all_to_all | solution.py:116
  134.2 12.6 %all-gather.5.cloned.1.call-start = ((), (), s32[]{:S(2)}) async-start(), calls=%async_computation.5 | async-start | bytes 2211840 | tf_op jit(solution)/shard_map/all_gather | solution.py:72
  135.2 82.7 %reduce-scatter.2.cloned.1.call-start = ((), (), s32[]{:S(2)}) async-start(), calls=%async_computation.6 | async-start | bytes 552960 | tf_op jit(solution)/shard_map/reduce_scatter | solution.py:127
  199.4 5.3 %copy-start.3 = (bf16[128,1440]{0,1:T(8,128)(2,1)S(1)}, bf16[128,1440]{0,1:T(8,128)(2,1)}, u32[]{:S(2)}) copy-start(bf16[128,1440]{0,1:T(8,128)(2,1)} %convolution_convert_fusion.2) | copy-start | bytes 1105924
Sparse Core Ops, SparseCore 0:
  8.9 14.5 all-gather.2
  27.2 26.4 all-reduce.2
  136.5 10.1 all-gather.4
  206.8 11.0 reduce-scatter.1
where the time goes:
time: 227 us; the launch traced here: 226 us
  waiting for transfers between devices  90.4 us (40%)
  blocking collectives  62 us (27%)
  local copies, waits for them, and re-layouts  23.6 us (10%)
  matrix products  16.9 us (7%)
  between operations  13.3 us (6%)
  other arithmetic  13.1 us (6%)
  starting transfers between devices  7.02 us (3%)
    all_to_all x1, blocking collectives, local(): lax.all_to_all(outgoing, ('expert', 'seq'), split_axis=0, concat_axis=0,...  59.3 us
    all_to_all x1, waiting for transfers between devices, local(): lax.all_to_all(expert_part.astype(jnp.bfloat16), ('expert', 'seq'), split...  39.1 us
    psum x1, waiting for transfers between devices, local(): lax.psum(attn_part.astype(jnp.bfloat16), 'tensor').astype(jnp.float32)  24.1 us
    reduce_scatter x1, waiting for transfers between devices, local(): lax.psum_scatter(combined.astype(jnp.bfloat16), 'tensor', scatter_dimensi...  11.2 us
    all_gather x1, waiting for transfers between devices, local(): lax.all_gather(shared_gate_up, 'seq', axis=0, tiled=True)  8.65 us
    all_gather x1, waiting for transfers between devices, local(): lax.all_gather(out_proj, 'seq', axis=1, tiled=True)  6.56 us
    gather x1, local copies, waits for them, and re-layouts, local(): returned.reshape(expert_count * capacity, width)[slots].astype(jnp.float32)  6.36 us
    dot_general x1, matrix products, local(): jnp.einsum('scd,dhf->schf', arrived, expert_gate_up[0], preferred_element...  6.02 us
  transfers between devices with their start and end apart: 6, of which 5 were waited for; matrix products, arithmetic and copies ran while one was open for 6% of the time, Pallas kernels for 0%

commit v1 on v0

--- a/solution.py
+++ b/solution.py
@@ -1,8 +1,11 @@
+import functools
 import math
 
 import jax
 import jax.numpy as jnp
 from jax import lax
+from jax.experimental import pallas as pl
+from jax.experimental.pallas import tpu as pltpu
 from jax.sharding import PartitionSpec as P
 
 WINDOW = 128
@@ -131,7 +134,399 @@
     return (stream_cols + summed).astype(jnp.bfloat16)
 
 
+MESH_ID = pl.DeviceIdType.MESH
+LANES = 128
+
+
+def pad_lanes(count):
+    return -(-count // LANES) * LANES
+
+
+def at_table(table, index):
+    value = jnp.int32(table[0])
+    for place in range(1, len(table)):
+        value = jnp.where(index == place, jnp.int32(table[place]), value)
+    return value
+
+
+def when(condition, action):
+    pl.when(condition)(action)
+
+
+def greet(others):
+    barrier = pltpu.get_barrier_semaphore()
+    for condition, device in others:
+        def send(device=device):
+            pl.semaphore_signal(barrier, inc=1, device_id=device, device_id_type=MESH_ID)
+        send() if condition is None else when(condition, send)
+    count = sum(jnp.int32(1) if condition is None else condition.astype(jnp.int32) for condition, _ in others)
+    pl.semaphore_wait(barrier, count)
+
+
+def remote(source, target, send_sem, recv_sem, device):
+    return pltpu.make_async_remote_copy(
+        src_ref=source, dst_ref=target, send_sem=send_sem, recv_sem=recv_sem,
+        device_id=device, device_id_type=MESH_ID,
+    )
+
+
+def front_kernel(
+    chips, q_ref, kv_ref, res_ref, sink_ref, gain_ref, proj_ref, sgu_ref, sdn_ref, ids_ref, gw_ref,
+    nbuf, stream_ref, sgu_out, sdn_out,
+    kv_prev, proj_other, ctx, part, xsend, xrecv,
+    wsend, wrecv, kvsem, xsem, gsend, grecv,
+):
+    e, s, t = lax.axis_index("expert"), lax.axis_index("seq"), lax.axis_index("tensor")
+    rows = q_ref.shape[0]
+    half_rows = rows // 2
+    col = proj_ref.shape[1]
+    depth = sgu_ref.shape[0]
+    width = 2 * col
+    core, across = {"seq": 1 - s}, {"tensor": 1 - t}
+    up, down = {"expert": e + 1}, {"expert": e - 1}
+    has_up, has_down = e < chips - 1, e > 0
+    greet([
+        (None, core), (None, across), (has_up, up), (has_down, down),
+        ((s == 1) & has_up, {"expert": e + 1, "seq": 0}),
+        ((s == 0) & has_down, {"expert": e - 1, "seq": 1}),
+    ])
+    first = (e == 0) & (s == 0)
+    kv_near = remote(kv_ref, kv_prev, kvsem.at[0], kvsem.at[1], core)
+    kv_far = remote(kv_ref, kv_prev, kvsem.at[0], kvsem.at[1], {"expert": e + 1, "seq": 0})
+    when(s == 0, lambda: kv_near.start())
+    when((s == 1) & has_up, lambda: kv_far.start())
+    weights = [
+        remote(proj_ref, proj_other, wsend.at[0], wrecv.at[0], core),
+        remote(sgu_ref, sgu_out.at[pl.ds(s * depth, depth)], wsend.at[1], wrecv.at[1], core),
+        remote(sdn_ref, sdn_out.at[s], wsend.at[2], wrecv.at[2], core),
+    ]
+    for copy in weights:
+        copy.start()
+    sgu_out[pl.ds(s * depth, depth), :] = sgu_ref[...]
+    sdn_out[s] = sdn_ref[...]
+
+    def blank():
+        kv_prev[...] = jnp.zeros_like(kv_prev)
+    when(first, blank)
+    when(jnp.logical_not(first), lambda: kv_near.wait_recv())
+
+    lane = lax.broadcasted_iota(jnp.int32, (rows, LANES), 1)
+    head = LANES // 2
+    low = lane < head
+    own_mask = lax.broadcasted_iota(jnp.int32, (rows, rows), 1) <= lax.broadcasted_iota(jnp.int32, (rows, rows), 0)
+    bias = jnp.where(first, -1e30, 0.0).astype(jnp.float32)
+    kv_count = kv_ref.shape[1] // LANES
+    pairs = q_ref.shape[1] // LANES // kv_count
+    inv = 1.0 / math.sqrt(head)
+
+    def halves(ref, group):
+        value = ref[:, group * LANES:(group + 1) * LANES].astype(jnp.float32)
+        turned = pltpu.roll(value, head, 1)
+        zero = jnp.zeros_like(value)
+        return [
+            jnp.where(low, value, zero).astype(jnp.bfloat16), jnp.where(low, zero, turned).astype(jnp.bfloat16),
+            jnp.where(low, turned, zero).astype(jnp.bfloat16), jnp.where(low, zero, value).astype(jnp.bfloat16),
+        ]
+
+    for group in range(kv_count):
+        mine, before = halves(kv_ref, group), halves(kv_prev, group)
+        keys = jnp.concatenate([mine[0], before[0], mine[1], before[1]], axis=0)
+        values = jnp.concatenate([mine[2], before[2], mine[3], before[3]], axis=0)
+        for pair in range(pairs):
+            place = group * pairs + pair
+            query = q_ref[:, place * LANES:(place + 1) * LANES]
+            scores = lax.dot_general(query, keys, (((1,), (1,)), ((), ())), preferred_element_type=jnp.float32)
+            pieces = []
+            for side in range(2):
+                sink = sink_ref[2 * place + side]
+                near = scores[:, 2 * side * rows:(2 * side + 1) * rows] * inv
+                far = scores[:, (2 * side + 1) * rows:(2 * side + 2) * rows] * inv + bias
+                score = jnp.where(own_mask, near, far)
+                top = jnp.maximum(jnp.max(score, axis=1, keepdims=True), sink)
+                expo = jnp.exp(score - top)
+                denom = jnp.sum(expo, axis=1, keepdims=True) + jnp.exp(sink - top)
+                weight = expo / denom
+                pieces.append(jnp.where(own_mask, weight, 0.0).astype(jnp.bfloat16))
+                pieces.append(jnp.where(own_mask, 0.0, weight).astype(jnp.bfloat16))
+            out = jnp.dot(jnp.concatenate(pieces, axis=1), values, preferred_element_type=jnp.float32)
+            ctx[:, place * LANES:(place + 1) * LANES] = out.astype(jnp.bfloat16)
+
+    mine = jnp.dot(ctx[...], proj_ref[...], preferred_element_type=jnp.float32)
+    weights[0].wait_recv()
+    other = jnp.dot(ctx[...], proj_other[...], preferred_element_type=jnp.float32)
+    part[...] = jnp.concatenate(
+        [jnp.where(s == 0, mine, other), jnp.where(s == 0, other, mine)], axis=1
+    )
+    xsend[...] = part[pl.ds((1 - t) * half_rows, half_rows), :].astype(jnp.bfloat16)
+    swap = remote(xsend, xrecv, xsem.at[0], xsem.at[1], across)
+    swap.start()
+    kept = part[pl.ds(t * half_rows, half_rows), :] + res_ref[pl.ds(t * half_rows, half_rows), :].astype(jnp.float32)
+    experts = chips * 2
+    ids = ids_ref[pl.ds(t * half_rows, half_rows), :]
+    gw = gw_ref[pl.ds(t * half_rows, half_rows), :]
+    base = width % LANES
+    lane_half = lax.broadcasted_iota(jnp.int32, (half_rows, LANES), 1)
+    gates = jnp.zeros((half_rows, LANES), jnp.float32)
+    for k in range(ids.shape[1]):
+        hit_high = lane_half == ids[:, k:k + 1] + base
+        hit_low = lane_half == ids[:, k:k + 1] + (base + experts)
+        value = gw[:, k:k + 1]
+        high = value.astype(jnp.bfloat16).astype(jnp.float32)
+        gates = gates + jnp.where(hit_high, high, 0.0) + jnp.where(hit_low, value - high, 0.0)
+    swap.wait_recv()
+    stream = kept + xrecv[...].astype(jnp.float32)
+    stream_ref[...] = stream
+    scale = lax.rsqrt(jnp.mean(stream * stream, axis=1, keepdims=True) + norm_eps)
+    normed = (stream * scale * gain_ref[...]).astype(jnp.bfloat16)
+    own = nbuf.at[e, s, t]
+    own[:, :width] = normed
+    edge = width // LANES * LANES
+    tile = own[:, edge:edge + LANES].astype(jnp.float32)
+    own[:, edge:edge + LANES] = jnp.where(lane_half < base, tile, gates).astype(jnp.bfloat16)
+
+    def piece(ee, ss, tt, way, device):
+        place = (ee * 2 + ss) * 2 + tt
+        return remote(nbuf.at[ee, ss, tt], nbuf.at[ee, ss, tt], gsend.at[way, place], grecv.at[place], device)
+
+    UP, DOWN, ACROSS, CORE = 0, 1, 2, 3
+    when(has_up, lambda: piece(e, s, t, UP, up).start())
+    when(has_down, lambda: piece(e, s, t, DOWN, down).start())
+    piece(e, s, t, ACROSS, across).start()
+    piece(e, s, t, CORE, core).start()
+
+    def from_across(ee):
+        got = piece(ee, s, 1 - t, CORE, core)
+        got.wait_recv()
+        got.start()
+
+    for d in range(1, chips):
+        def from_below(d=d):
+            piece(e - d, s, t, UP, up).wait_recv()
+            when(has_up, lambda: piece(e - d, s, t, UP, up).start())
+            piece(e - d, s, t, ACROSS, across).start()
+            piece(e - d, s, t, CORE, core).start()
+        def from_above(d=d):
+            piece(e + d, s, t, DOWN, down).wait_recv()
+            when(has_down, lambda: piece(e + d, s, t, DOWN, down).start())
+            piece(e + d, s, t, ACROSS, across).start()
+            piece(e + d, s, t, CORE, core).start()
+        when(e - d >= 0, from_below)
+        when(e + d < chips, from_above)
+        if d == 1:
+            from_across(e)
+        else:
+            when(e - d + 1 >= 0, lambda d=d: from_across(e - d + 1))
+            when(e + d - 1 < chips, lambda d=d: from_across(e + d - 1))
+    d = chips - 1
+    when(e - d >= 0, lambda: from_across(e - d))
+    when(e + d < chips, lambda: from_across(e + d))
+    for ee in range(chips):
+        for tt in range(2):
+            piece(ee, 1 - s, tt, CORE, core).wait_recv()
+    for copy in weights[1:]:
+        copy.wait_recv()
+    for ee in range(chips):
+        piece(ee, s, t, ACROSS, across).wait_send()
+        piece(ee, s, t, CORE, core).wait_send()
+        piece(ee, s, 1 - t, CORE, core).wait_send()
+        when(has_up & (e >= ee), lambda ee=ee: piece(ee, s, t, UP, up).wait_send())
+        when(has_down & (e <= ee), lambda ee=ee: piece(ee, s, t, DOWN, down).wait_send())
+    for copy in weights:
+        copy.wait_send()
+    swap.wait_send()
+    when(s == 0, lambda: kv_near.wait_send())
+    when((s == 1) & has_up, lambda: kv_far.wait_send())
+
+
+def back_kernel(
+    chips, hidden_ref, down_ref, gate_ref, sh_ref, sdn_ref, stream_ref, out_ref,
+    keep, dsend, drecv, xkeep, xsend, xrecv, zsend, zrecv,
+    dsem_s, dsem_r, xsem_s, xsem_r, zsem_s, zsem_r,
+):
+    e, s, t = lax.axis_index("expert"), lax.axis_index("seq"), lax.axis_index("tensor")
+    rows, col = out_ref.shape
+    half_rows = rows // 2
+    width = 2 * col
+    base = width % LANES
+    experts = 2 * chips
+    core, across = {"seq": 1 - s}, {"tensor": 1 - t}
+    up, down = {"expert": e + 1}, {"expert": e - 1}
+    has_up, has_down = e < chips - 1, e > 0
+    greet([(None, core), (None, across), (has_up, up), (has_down, down)])
+    expert = e * 2 + s
+    lane = lax.broadcasted_iota(jnp.int32, (rows, LANES), 1)
+    wanted = (lane == base + expert) | (lane == base + experts + expert)
+    order = [sorted(range(chips), key=lambda dest, me=me: -abs(dest - me)) for me in range(chips)]
+    dests = [at_table([order[me][k] for me in range(chips)], e) for k in range(chips)]
+
+    def block(dest, core_index):
+        start = pl.multiple_of((dest * 2 + core_index) * rows, rows)
+        gate = jnp.sum(
+            jnp.where(wanted, gate_ref[pl.ds(start, rows), :].astype(jnp.float32), 0.0), axis=1, keepdims=True
+        )
+        return gate * jnp.dot(
+            hidden_ref[pl.ds(start, rows), :], down_ref[...], preferred_element_type=jnp.float32
+        )
+
+    def to_core(k):
+        return remote(dsend.at[k], drecv.at[k], dsem_s.at[k], dsem_r.at[k], core)
+
+    def to_across(k):
+        return remote(xsend.at[k], xrecv.at[k], xsem_s.at[k], xsem_r.at[k], across)
+
+    def to_up(k):
+        dest = dests[k]
+        return remote(zsend.at[k], zrecv.at[0, dest], zsem_s.at[k], zsem_r.at[0, dest], up)
+
+    def to_down(k):
+        dest = dests[k]
+        return remote(zsend.at[k], zrecv.at[1, dest], zsem_s.at[k], zsem_r.at[1, dest], down)
+
+    def stage_a(k):
+        dsend[k] = block(dests[k], 1 - s).astype(jnp.bfloat16)
+        to_core(k).start()
+        value = block(dests[k], s)
+        keep[k] = value
+        if k == chips - 1:
+            shared = jnp.concatenate([
+                jnp.dot(sh_ref[...], sdn_ref[h], preferred_element_type=jnp.float32) for h in range(2)
+            ], axis=1)
+            keep[k] += shared
+            keep[k, pl.ds(t * half_rows, half_rows), :] += stream_ref[...]
+
+    def stage_b(k):
+        to_core(k).wait_recv()
+        total = keep[k] + drecv[k].astype(jnp.float32)
+        left, right = total[:, :col], total[:, col:]
+        xsend[k] = jnp.where(t == 0, right, left).astype(jnp.bfloat16)
+        to_across(k).start()
+        xkeep[k] = jnp.where(t == 0, left, right)
+
+    def stage_c(k):
+        dest = dests[k]
+        to_across(k).wait_recv()
+        xkeep[k] += xrecv[k].astype(jnp.float32)
+
+        def take(side, device_of):
+            device_of(k).wait_recv()
+            xkeep[k] += zrecv[side, dest].astype(jnp.float32)
+        if k < chips - 1:
+            when((dest > e) & has_down, lambda: take(0, to_up))
+            when((dest < e) & has_up, lambda: take(1, to_down))
+            zsend[k] = xkeep[k].astype(jnp.bfloat16)
+            when(dest > e, lambda: to_up(k).start())
+            when(dest < e, lambda: to_down(k).start())
+        else:
+            when(has_down, lambda: take(0, to_up))
+            when(has_up, lambda: take(1, to_down))
+            out_ref[...] = xkeep[k].astype(jnp.bfloat16)
+
+    for step in range(chips + 2):
+        if step < chips:
+            stage_a(step)
+        if 0 <= step - 1 < chips:
+            stage_b(step - 1)
+        if 0 <= step - 2 < chips:
+            stage_c(step - 2)
+    for k in range(chips):
+        to_core(k).wait_send()
+        to_across(k).wait_send()
+        if k < chips - 1:
+            to_up(k).wait_send()
+
+
+def gathered(
+    queries, keys_values, residual, sink_logits, norm_gain, out_proj, shared_gate_up, shared_down,
+    expert_gate_up, expert_down, expert_ids, gate_weights,
+):
+    chips = lax.axis_size("expert")
+    rows, width = residual.shape
+    col = out_proj.shape[1]
+    inner = out_proj.shape[0]
+    depth = shared_gate_up.shape[0]
+    sff = shared_gate_up.shape[2]
+    wide = pad_lanes(width)
+    kv_flat = keys_values.reshape(rows, -1)
+    sgu = shared_gate_up.reshape(depth, 2 * sff)
+    vmem = pl.BlockSpec(memory_space=pltpu.VMEM)
+    smem = pl.BlockSpec(memory_space=pltpu.SMEM)
+    bf16, f32 = jnp.bfloat16, jnp.float32
+    dma = pltpu.SemaphoreType.DMA
+    pieces = 4 * chips
+    nbuf, stream, sgu_full, sdn_full = pl.pallas_call(
+        functools.partial(front_kernel, chips),
+        name="front",
+        out_shape=(
+            jax.ShapeDtypeStruct((chips, 2, 2, rows // 2, wide), bf16),
+            jax.ShapeDtypeStruct((rows // 2, width), f32),
+            jax.ShapeDtypeStruct((2 * depth, 2 * sff), bf16),
+            jax.ShapeDtypeStruct((2, sff, col), bf16),
+        ),
+        in_specs=[vmem, vmem, vmem, smem] + [vmem] * 6,
+        out_specs=(vmem,) * 4,
+        scratch_shapes=[
+            pltpu.VMEM(kv_flat.shape, bf16),
+            pltpu.VMEM((inner, col), bf16),
+            pltpu.VMEM((rows, inner), bf16),
+            pltpu.VMEM((rows, width), f32),
+            pltpu.VMEM((rows // 2, width), bf16),
+            pltpu.VMEM((rows // 2, width), bf16),
+            dma((3,)), dma((3,)), dma((2,)), dma((2,)), dma((4, pieces)), dma((pieces,)),
+        ],
+        compiler_params=pltpu.CompilerParams(
+            collective_id=0, has_side_effects=True, vmem_limit_bytes=40 * 1024 * 1024
+        ),
+    )(queries, kv_flat, residual, sink_logits, norm_gain.reshape(1, -1), out_proj, sgu, shared_down,
+      expert_ids, gate_weights)
+    flat = nbuf.reshape(2 * chips * rows, wide)
+    tokens = flat[:, :width]
+    pre = jnp.einsum("pd,dhf->phf", tokens, expert_gate_up[0], preferred_element_type=f32)
+    hidden = glu_act(pre[:, 0], pre[:, 1]).astype(bf16)
+    block_index = lax.axis_index(("expert", "seq"))
+    here = lax.dynamic_slice_in_dim(flat, block_index * rows, rows, 0)[:, :width]
+    shared_pre = jnp.dot(here, sgu_full, preferred_element_type=f32)
+    shared_hidden = glu_act(shared_pre[:, :sff], shared_pre[:, sff:]).astype(bf16)
+    edge = width // LANES * LANES
+    return pl.pallas_call(
+        functools.partial(back_kernel, chips),
+        name="back",
+        out_shape=jax.ShapeDtypeStruct((rows, col), bf16),
+        in_specs=[vmem] * 6,
+        out_specs=vmem,
+        scratch_shapes=[
+            pltpu.VMEM((chips, rows, width), f32),
+            pltpu.VMEM((chips, rows, width), bf16),
+            pltpu.VMEM((chips, rows, width), bf16),
+            pltpu.VMEM((chips, rows, col), f32),
+            pltpu.VMEM((chips, rows, col), bf16),
+            pltpu.VMEM((chips, rows, col), bf16),
+            pltpu.VMEM((chips, rows, col), bf16),
+            pltpu.VMEM((2, chips, rows, col), bf16),
+            dma((chips,)), dma((chips,)), dma((chips,)), dma((chips,)), dma((chips,)), dma((2, chips)),
+        ],
+        compiler_params=pltpu.CompilerParams(
+            collective_id=1, has_side_effects=True, vmem_limit_bytes=40 * 1024 * 1024
+        ),
+    )(hidden, expert_down[0], flat[:, edge:edge + LANES], shared_hidden, sdn_full, stream)
+
+
+def fits(mesh, rows, width, top):
+    devices = mesh.shape["expert"] * mesh.shape["seq"]
+    capacity = max(2, 3 * rows * top // (2 * devices))
+    spare = pad_lanes(width) - width
+    return (
+        rows <= 2 * capacity and rows == WINDOW and mesh.shape["tensor"] == 2 and mesh.shape["seq"] == 2
+        and spare >= 2 * devices
+    )
+
+
 def solution(mesh):
+    def body(*args):
+        residual, expert_ids, gate_up = args[2], args[10], args[8]
+        if gate_up.shape[0] == 1 and fits(mesh, residual.shape[0], residual.shape[1], expert_ids.shape[1]):
+            return gathered(*args)
+        return local(*args)
+
     in_specs = (
         P(("group", "expert", "seq"), "tensor"),
         P(("group", "expert", "seq"), "tensor", None),
@@ -147,4 +542,4 @@
         P(("group", "expert", "seq"), None),
     )
     out_specs = P(("group", "expert", "seq"), "tensor")
-    return jax.shard_map(local, mesh=mesh, in_specs=in_specs, out_specs=out_specs, check_vma=False)
+    return jax.shard_map(body, mesh=mesh, in_specs=in_specs, out_specs=out_specs, check_vma=False)

time: 227 us -> 84.3 us (0.37)
  the two profiles are of different devices: /device:TPU:0 before, /device:TPU:16 now
where the time goes in v1:
time: 84.3 us; the launch traced here: 83.9 us
  Pallas kernels  65.4 us (78%)
  local copies, waits for them, and re-layouts  12 us (14%)
  matrix products  5.4 us (6%)
  other arithmetic  0.95 us (1%)
    pallas_call x1, Pallas kernels, gathered(): pl.pallas_call(functools.partial(back_kernel, chips), name='back', out_sh...  32.8 us
    pallas_call x1, Pallas kernels, gathered(): pl.pallas_call(functools.partial(front_kernel, chips), name='front', out_...  32.7 us
    unnamed x17, local copies, waits for them, and re-layouts  9.81 us
    dot_general x1, matrix products, gathered(): jnp.einsum('pd,dhf->phf', tokens, expert_gate_up[0], preferred_element_ty...  5.03 us

profile of v1, /device:TPU:16, one launch (start us, length us, event | category | flops | bytes accessed | tf_op | source)
XLA Modules:
  0.0 83.9 jit_solution(2461496426514791300)
XLA Ops:
  0.0 1.3 %reshape.20.gain_ref = f32[1,1440]{1,0:T(1,128)} reshape(f32[1440]{0:T(1024)} %param.16) | data formatting | bytes 11520 | tf_op jit(solution)/shard_map/reshape | solution.py:479
  1.3 0.0 copy-start.1
  1.3 0.9 %copy.31 = bf16[16,8,2,128]{3,1,2,0:T(8,128)(2,1)S(1)} copy(bf16[16,8,2,128]{3,2,1,0:T(2,128)(2,1)} %bitcast.22) | data formatting | bytes 131072
  2.2 0.8 copy.16.ids_ref
  3.0 0.8 copy.17.gw_ref
  3.8 1.2 %copy.13.res_ref = bf16[128,1440]{1,0:T(8,128)(2,1)S(1)} copy(bf16[128,1440]{0,1:T(8,128)(2,1)} %param.14) | data formatting | bytes 737280 | tf_op args[2]
  4.9 1.2 %copy.15.sdn_ref = bf16[256,720]{1,0:T(8,128)(2,1)S(1)} copy(bf16[256,720]{0,1:T(8,128)(2,1)} %param.19) | data formatting | bytes 737280 | tf_op args[7]
  6.1 1.3 %copy.27 = bf16[90,8,2,256]{3,1,2,0:T(8,128)(2,1)S(1)} copy(bf16[90,8,2,256]{3,2,1,0:T(2,128)(2,1)} %bitcast.21) | data formatting | bytes 1474560
  7.4 1.7 %copy.14.proj_ref = bf16[1024,720]{1,0:T(8,128)(2,1)S(1)} copy(bf16[1024,720]{0,1:T(8,128)(2,1)} %param.17) | data formatting | bytes 2949120 | tf_op args[5]
  9.1 0.0 copy-done.1
  9.1 0.0 copy-start.2
  9.1 0.7 copy-done.2
  9.8 0.0 copy-start.3
  9.8 0.7 copy-done.3
  10.4 0.0 copy-start.4
  10.4 32.7 %front.1 = (bf16[4,2,2,64,1536]{4,3,2,1,0:T(8,128)(2,1)S(1)}, f32[64,1440]{1,0:T(8,128)S(1)}, bf16[1440,512]{1,0:T(8,128)(2,1)S(1)}, bf16[2,256,720]{2,1,0:T(8,128)(2,1)S(1)}) custom-call(bf16[128,1024]{1,0:T(8,128)(2,1)S(1)} %copy-done.1, bf16[128,256]{1,0:T(8,128)(2,1)S(1)} %bitcast.17, bf16[128,1440]{1,0:T(8,128)(2,1)S(1)} %copy.13.res_ref, ...), custom_call_target="tpu_custom_call" | custom-call | tf_op jit(solution)/shard_map/front/pallas_call | solution.py:456
  43.1 0.4 fusion.6
  43.6 0.0 copy-done.4
  43.6 5.0 %fusion = f32[1024,2,720]{2,0,1:T(8,128)S(1)} fusion(bf16[1440,2,720]{2,1,0:T(2,128)(2,1)S(1)} %bitcast.23, bf16[1024,1536]{1,0:T(8,128)(2,1)S(1)} %bitcast.20), kind=kOutput, calls=%fused_computation | convolution fusion | flops 4246732800 | bytes 13191168 | tf_op jit(solution)/shard_map/pd,dhf->phf/dot_general | solution.py:483
  48.6 0.0 copy-start
  48.6 0.9 %fusion.5.hidden_ref = bf16[1024,720]{1,0:T(8,128)(2,1)S(1)} fusion(f32[1024,2,720]{2,0,1:T(8,128)S(1)} %fusion), kind=kLoop, calls=%fused_computation.7 | loop fusion | flops 5898240 | bytes 7372800 | tf_op jit(solution)/shard_map/convert_element_type | solution.py:484
  49.5 0.7 copy-done
  50.3 32.8 %back.1 = bf16[128,720]{1,0:T(8,128)(2,1)S(1)} custom-call(bf16[1024,720]{1,0:T(8,128)(2,1)S(1)} %fusion.5.hidden_ref, bf16[720,1440]{1,0:T(8,128)(2,1)S(1)} %bitcast.16, bf16[1024,128]{1,0:T(8,128)(2,1)S(1)} %slice.31.gate_ref, bf16[128,256]{1,0:T(8,128)(2,1)S(1)} %fusion.10.sh_ref, bf16[2,256,720]{2,1,0:T(8,128)(2,1)S(1)} %get-tuple-element.11.sdn_ref, ...), custom_call_target="tpu_custom_call" | custom-call | tf_op jit(solution)/shard_map/back/pallas_call | solution.py:490
  83.0 0.8 copy.22
  (2 shorter events, 0.1 us)
Async XLA Ops:
  1.3 7.8 %copy-start.1 = (bf16[128,1024]{1,0:T(8,128)(2,1)S(1)}, bf16[128,1024]{1,0:T(8,128)(2,1)}, u32[]{:S(2)}) copy-start(bf16[128,1024]{1,0:T(8,128)(2,1)} %q_ref.1) | copy-start | bytes 786436
  9.1 0.7 copy-start.2
  9.8 0.7 copy-start.3
  10.4 33.1 %copy-start.4 = (bf16[1,1440,2,720]{3,2,1,0:T(2,128)(2,1)S(1)}, bf16[1,1440,2,720]{3,2,1,0:T(2,128)(2,1)}, u32[]{:S(2)}) copy-start(bf16[1,1440,2,720]{3,2,1,0:T(2,128)(2,1)} %param.20) | copy-start | bytes 12441604
  48.6 1.6 %copy-start = (bf16[1,720,1440]{2,1,0:T(8,128)(2,1)S(1)}, bf16[1,720,1440]{2,1,0:T(8,128)(2,1)}, u32[]{:S(2)}) copy-start(bf16[1,720,1440]{2,1,0:T(8,128)(2,1)} %param.21) | copy-start | bytes 6220804

commit v2 on v1

--- a/solution.py
+++ b/solution.py
@@ -136,6 +136,7 @@
 
 MESH_ID = pl.DeviceIdType.MESH
 LANES = 128
+CHUNKS = 2
 
 
 def pad_lanes(count):
@@ -173,13 +174,13 @@
 def front_kernel(
     chips, q_ref, kv_ref, res_ref, sink_ref, gain_ref, proj_ref, sgu_ref, sdn_ref, ids_ref, gw_ref,
     nbuf, stream_ref, sgu_out, sdn_out,
-    kv_prev, proj_other, ctx, part, xsend, xrecv,
-    wsend, wrecv, kvsem, xsem, gsend, grecv,
+    kv_prev, proj_other, ctx, part, xsend, xrecv, gscr,
+    wsend, wrecv, kvsem, xsem, own_sem, gsend, grecv,
 ):
     e, s, t = lax.axis_index("expert"), lax.axis_index("seq"), lax.axis_index("tensor")
     rows = q_ref.shape[0]
     half_rows = rows // 2
-    col = proj_ref.shape[1]
+    col = proj_ref.shape[0]
     depth = sgu_ref.shape[0]
     width = 2 * col
     core, across = {"seq": 1 - s}, {"tensor": 1 - t}
@@ -202,7 +203,8 @@
     ]
     for copy in weights:
         copy.start()
-    sgu_out[pl.ds(s * depth, depth), :] = sgu_ref[...]
+    own_sgu = pltpu.make_async_copy(sgu_ref, sgu_out.at[pl.ds(s * depth, depth)], own_sem)
+    own_sgu.start()
     sdn_out[s] = sdn_ref[...]
 
     def blank():
@@ -215,12 +217,15 @@
     low = lane < head
     own_mask = lax.broadcasted_iota(jnp.int32, (rows, rows), 1) <= lax.broadcasted_iota(jnp.int32, (rows, rows), 0)
     bias = jnp.where(first, -1e30, 0.0).astype(jnp.float32)
-    kv_count = kv_ref.shape[1] // LANES
+    kv_count = kv_ref.shape[0] // rows
+    to_row = lax.broadcasted_iota(jnp.int32, (kv_count * rows, kv_count * rows), 0)
+    from_row = lax.broadcasted_iota(jnp.int32, (kv_count * rows, kv_count * rows), 1)
+    sort_groups = (from_row == (to_row % rows) * kv_count + to_row // rows).astype(jnp.bfloat16)
     pairs = q_ref.shape[1] // LANES // kv_count
     inv = 1.0 / math.sqrt(head)
 
-    def halves(ref, group):
-        value = ref[:, group * LANES:(group + 1) * LANES].astype(jnp.float32)
+    def halves(whole, group):
+        value = whole[group * rows:(group + 1) * rows]
         turned = pltpu.roll(value, head, 1)
         zero = jnp.zeros_like(value)
         return [
@@ -228,8 +233,10 @@
             jnp.where(low, turned, zero).astype(jnp.bfloat16), jnp.where(low, zero, value).astype(jnp.bfloat16),
         ]
 
+    kv_mine = jnp.dot(sort_groups, kv_ref[...], preferred_element_type=jnp.float32)
+    kv_before = jnp.dot(sort_groups, kv_prev[...], preferred_element_type=jnp.float32)
     for group in range(kv_count):
-        mine, before = halves(kv_ref, group), halves(kv_prev, group)
+        mine, before = halves(kv_mine, group), halves(kv_before, group)
         keys = jnp.concatenate([mine[0], before[0], mine[1], before[1]], axis=0)
         values = jnp.concatenate([mine[2], before[2], mine[3], before[3]], axis=0)
         for pair in range(pairs):
@@ -251,86 +258,112 @@
             out = jnp.dot(jnp.concatenate(pieces, axis=1), values, preferred_element_type=jnp.float32)
             ctx[:, place * LANES:(place + 1) * LANES] = out.astype(jnp.bfloat16)
 
-    mine = jnp.dot(ctx[...], proj_ref[...], preferred_element_type=jnp.float32)
+    along = (((1,), (1,)), ((), ()))
+    mine = lax.dot_general(ctx[...], proj_ref[...], along, preferred_element_type=jnp.float32)
     weights[0].wait_recv()
-    other = jnp.dot(ctx[...], proj_other[...], preferred_element_type=jnp.float32)
+    other = lax.dot_general(ctx[...], proj_other[...], along, preferred_element_type=jnp.float32)
     part[...] = jnp.concatenate(
         [jnp.where(s == 0, mine, other), jnp.where(s == 0, other, mine)], axis=1
     )
     xsend[...] = part[pl.ds((1 - t) * half_rows, half_rows), :].astype(jnp.bfloat16)
     swap = remote(xsend, xrecv, xsem.at[0], xsem.at[1], across)
     swap.start()
-    kept = part[pl.ds(t * half_rows, half_rows), :] + res_ref[pl.ds(t * half_rows, half_rows), :].astype(jnp.float32)
+    picked_row = lax.broadcasted_iota(jnp.int32, (half_rows, rows), 0) + t * half_rows
+    pick = (lax.broadcasted_iota(jnp.int32, (half_rows, rows), 1) == picked_row).astype(jnp.bfloat16)
+    kept = part[pl.ds(t * half_rows, half_rows), :] + lax.dot_general(
+        pick, res_ref[...], along, preferred_element_type=jnp.float32
+    )
     experts = chips * 2
-    ids = ids_ref[pl.ds(t * half_rows, half_rows), :]
-    gw = gw_ref[pl.ds(t * half_rows, half_rows), :]
     base = width % LANES
     lane_half = lax.broadcasted_iota(jnp.int32, (half_rows, LANES), 1)
-    gates = jnp.zeros((half_rows, LANES), jnp.float32)
-    for k in range(ids.shape[1]):
-        hit_high = lane_half == ids[:, k:k + 1] + base
-        hit_low = lane_half == ids[:, k:k + 1] + (base + experts)
-        value = gw[:, k:k + 1]
+    line = lax.broadcasted_iota(jnp.int32, (LANES, rows), 0)
+    gates = jnp.zeros((LANES, rows), jnp.float32)
+    for k in range(ids_ref.shape[0]):
+        ids = ids_ref[k:k + 1, :] + base
+        value = gw_ref[k:k + 1, :]
         high = value.astype(jnp.bfloat16).astype(jnp.float32)
-        gates = gates + jnp.where(hit_high, high, 0.0) + jnp.where(hit_low, value - high, 0.0)
+        gates = gates + jnp.where(line == ids, high, 0.0) + jnp.where(line == ids + experts, value - high, 0.0)
+    gscr[...] = gates.T
     swap.wait_recv()
     stream = kept + xrecv[...].astype(jnp.float32)
     stream_ref[...] = stream
     scale = lax.rsqrt(jnp.mean(stream * stream, axis=1, keepdims=True) + norm_eps)
-    normed = (stream * scale * gain_ref[...]).astype(jnp.bfloat16)
-    own = nbuf.at[e, s, t]
-    own[:, :width] = normed
+    normed = (stream * scale * gain_ref[...].reshape(1, width)).astype(jnp.bfloat16)
     edge = width // LANES * LANES
-    tile = own[:, edge:edge + LANES].astype(jnp.float32)
-    own[:, edge:edge + LANES] = jnp.where(lane_half < base, tile, gates).astype(jnp.bfloat16)
-
-    def piece(ee, ss, tt, way, device):
-        place = (ee * 2 + ss) * 2 + tt
-        return remote(nbuf.at[ee, ss, tt], nbuf.at[ee, ss, tt], gsend.at[way, place], grecv.at[place], device)
+    size = half_rows // CHUNKS
+
+    def piece(ee, ss, tt, c, way, device):
+        place = ((ee * 2 + ss) * 2 + tt) * CHUNKS + c
+        part_of = nbuf.at[ee, ss, tt, c]
+        return remote(part_of, part_of, gsend.at[way, place], grecv.at[place], device)
 
     UP, DOWN, ACROSS, CORE = 0, 1, 2, 3
-    when(has_up, lambda: piece(e, s, t, UP, up).start())
-    when(has_down, lambda: piece(e, s, t, DOWN, down).start())
-    piece(e, s, t, ACROSS, across).start()
-    piece(e, s, t, CORE, core).start()
-
-    def from_across(ee):
-        got = piece(ee, s, 1 - t, CORE, core)
+    edge_gates = gscr[pl.ds(t * half_rows, half_rows), :]
+    edge_tile = jnp.concatenate([normed[:, edge:], jnp.zeros((half_rows, edge + LANES - width), jnp.bfloat16)], axis=1)
+    edge_tile = jnp.where(lane_half < base, edge_tile.astype(jnp.float32), edge_gates).astype(jnp.bfloat16)
+    for c in range(CHUNKS):
+        nbuf[e, s, t, c, :, :edge] = normed[c * size:(c + 1) * size, :edge]
+        nbuf[e, s, t, c, :, edge:edge + LANES] = edge_tile[c * size:(c + 1) * size]
+        piece(e, s, t, c, ACROSS, across).start()
+        when(has_up, lambda c=c: piece(e, s, t, c, UP, up).start())
+        when(has_down, lambda c=c: piece(e, s, t, c, DOWN, down).start())
+        piece(e, s, t, c, CORE, core).start()
+
+    def own_column(d):
+        for c in range(CHUNKS):
+            def from_below(c=c):
+                piece(e - d, s, t, c, UP, up).wait_recv()
+                when(has_up, lambda: piece(e - d, s, t, c, UP, up).start())
+                if d > 1:
+                    piece(e - d, s, t, c, ACROSS, across).start()
+                piece(e - d, s, t, c, CORE, core).start()
+
+            def from_above(c=c):
+                piece(e + d, s, t, c, DOWN, down).wait_recv()
+                when(has_down, lambda: piece(e + d, s, t, c, DOWN, down).start())
+                if d > 1:
+                    piece(e + d, s, t, c, ACROSS, across).start()
+                piece(e + d, s, t, c, CORE, core).start()
+            when(e - d >= 0, from_below)
+            when(e + d < chips, from_above)
+
+    def take(ee, c):
+        got = piece(ee, s, 1 - t, c, CORE, core)
         got.wait_recv()
         got.start()
 
+    def other_column(d):
+        for c in range(CHUNKS):
+            when(e - d >= 0, lambda c=c: take(e - d, c))
+            when(e + d < chips, lambda c=c: take(e + d, c))
+
     for d in range(1, chips):
-        def from_below(d=d):
-            piece(e - d, s, t, UP, up).wait_recv()
-            when(has_up, lambda: piece(e - d, s, t, UP, up).start())
-            piece(e - d, s, t, ACROSS, across).start()
-            piece(e - d, s, t, CORE, core).start()
-        def from_above(d=d):
-            piece(e + d, s, t, DOWN, down).wait_recv()
-            when(has_down, lambda: piece(e + d, s, t, DOWN, down).start())
-            piece(e + d, s, t, ACROSS, across).start()
-            piece(e + d, s, t, CORE, core).start()
-        when(e - d >= 0, from_below)
-        when(e + d < chips, from_above)
+        own_column(d)
         if d == 1:
-            from_across(e)
+            for c in range(CHUNKS):
+                take(e, c)
+                when(has_up, lambda c=c: piece(e, s, 1 - t, c, UP, up).start())
+                when(has_down, lambda c=c: piece(e, s, 1 - t, c, DOWN, down).start())
         else:
-            when(e - d + 1 >= 0, lambda d=d: from_across(e - d + 1))
-            when(e + d - 1 < chips, lambda d=d: from_across(e + d - 1))
-    d = chips - 1
-    when(e - d >= 0, lambda: from_across(e - d))
-    when(e + d < chips, lambda: from_across(e + d))
+            other_column(d - 1)
+    other_column(chips - 1)
     for ee in range(chips):
         for tt in range(2):
-            piece(ee, 1 - s, tt, CORE, core).wait_recv()
+            for c in range(CHUNKS):
+                piece(ee, 1 - s, tt, c, CORE, core).wait_recv()
+    own_sgu.wait()
     for copy in weights[1:]:
         copy.wait_recv()
-    for ee in range(chips):
-        piece(ee, s, t, ACROSS, across).wait_send()
-        piece(ee, s, t, CORE, core).wait_send()
-        piece(ee, s, 1 - t, CORE, core).wait_send()
-        when(has_up & (e >= ee), lambda ee=ee: piece(ee, s, t, UP, up).wait_send())
-        when(has_down & (e <= ee), lambda ee=ee: piece(ee, s, t, DOWN, down).wait_send())
+    for c in range(CHUNKS):
+        for ee in range(chips):
+            near = (e == ee - 1) | (e == ee + 1)
+            when(jnp.logical_not(near), lambda ee=ee, c=c: piece(ee, s, t, c, ACROSS, across).wait_send())
+            piece(ee, s, t, c, CORE, core).wait_send()
+            piece(ee, s, 1 - t, c, CORE, core).wait_send()
+            when(has_up & (e >= ee), lambda ee=ee, c=c: piece(ee, s, t, c, UP, up).wait_send())
+            when(has_down & (e <= ee), lambda ee=ee, c=c: piece(ee, s, t, c, DOWN, down).wait_send())
+        when(has_up, lambda c=c: piece(e, s, 1 - t, c, UP, up).wait_send())
+        when(has_down, lambda c=c: piece(e, s, 1 - t, c, DOWN, down).wait_send())
     for copy in weights:
         copy.wait_send()
     swap.wait_send()
@@ -340,8 +373,8 @@
 
 def back_kernel(
     chips, hidden_ref, down_ref, gate_ref, sh_ref, sdn_ref, stream_ref, out_ref,
-    keep, dsend, drecv, xkeep, xsend, xrecv, zsend, zrecv,
-    dsem_s, dsem_r, xsem_s, xsem_r, zsem_s, zsem_r,
+    keep, dsend, drecv, xkeep, xsend, xrecv, zsend, zrecv, orecv, spare,
+    dsem_s, dsem_r, xsem_s, xsem_r, zsem_s, zsem_r, osem_r,
 ):
     e, s, t = lax.axis_index("expert"), lax.axis_index("seq"), lax.axis_index("tensor")
     rows, col = out_ref.shape
@@ -356,8 +389,16 @@
     expert = e * 2 + s
     lane = lax.broadcasted_iota(jnp.int32, (rows, LANES), 1)
     wanted = (lane == base + expert) | (lane == base + experts + expert)
-    order = [sorted(range(chips), key=lambda dest, me=me: -abs(dest - me)) for me in range(chips)]
-    dests = [at_table([order[me][k] for me in range(chips)], e) for k in range(chips)]
+    far_first = [sorted(range(chips), key=lambda dest, me=me: -abs(dest - me)) for me in range(chips)]
+    near_first = [
+        sorted(range(chips), key=lambda dest, me=me: (dest == me, abs(dest - me) != 1, -abs(dest - me)))
+        for me in range(chips)
+    ]
+    later = [at_table([far_first[me][k] for me in range(chips)], e) for k in range(chips)]
+    sooner = [at_table([near_first[me][k] for me in range(chips)], e) for k in range(chips)]
+    size = rows // CHUNKS
+    parts = [pl.ds(c * size, size) for c in range(CHUNKS)]
+    along = (((1,), (1,)), ((), ()))
 
     def block(dest, core_index):
         start = pl.multiple_of((dest * 2 + core_index) * rows, rows)
@@ -368,71 +409,100 @@
             hidden_ref[pl.ds(start, rows), :], down_ref[...], preferred_element_type=jnp.float32
         )
 
-    def to_core(k):
-        return remote(dsend.at[k], drecv.at[k], dsem_s.at[k], dsem_r.at[k], core)
-
-    def to_across(k):
-        return remote(xsend.at[k], xrecv.at[k], xsem_s.at[k], xsem_r.at[k], across)
-
-    def to_up(k):
-        dest = dests[k]
-        return remote(zsend.at[k], zrecv.at[0, dest], zsem_s.at[k], zsem_r.at[0, dest], up)
-
-    def to_down(k):
-        dest = dests[k]
-        return remote(zsend.at[k], zrecv.at[1, dest], zsem_s.at[k], zsem_r.at[1, dest], down)
-
-    def stage_a(k):
-        dsend[k] = block(dests[k], 1 - s).astype(jnp.bfloat16)
-        to_core(k).start()
-        value = block(dests[k], s)
-        keep[k] = value
-        if k == chips - 1:
+    def near_dest(dest):
+        return (dest == e + 1) | (dest == e - 1)
+
+    def to_core(dest):
+        return remote(dsend.at[dest], drecv.at[dest], dsem_s.at[dest], dsem_r.at[dest], core)
+
+    def to_across(dest, c):
+        return remote(
+            xsend.at[dest, parts[c]], xrecv.at[dest, parts[c]], xsem_s.at[dest, c], xsem_r.at[dest, c], across
+        )
+
+    def along_z(dest, side, c):
+        return remote(
+            zsend.at[dest, parts[c]], zrecv.at[side, dest, parts[c]], zsem_s.at[dest, c], zsem_r.at[side, dest, c],
+            down if side else up,
+        )
+
+    def other_z(dest, side, c):
+        return remote(
+            xsend.at[dest, parts[c]], orecv.at[side, parts[c]], xsem_s.at[dest, c], osem_r.at[side, c],
+            down if side else up,
+        )
+
+    def stage_a(dest, last):
+        dsend[dest] = block(dest, 1 - s).astype(jnp.bfloat16)
+        to_core(dest).start()
+        value = block(dest, s)
+        keep[dest] = value
+        if last:
             shared = jnp.concatenate([
-                jnp.dot(sh_ref[...], sdn_ref[h], preferred_element_type=jnp.float32) for h in range(2)
+                lax.dot_general(sh_ref[...], sdn_ref[h], along, preferred_element_type=jnp.float32) for h in range(2)
             ], axis=1)
-            keep[k] += shared
-            keep[k, pl.ds(t * half_rows, half_rows), :] += stream_ref[...]
-
-    def stage_b(k):
-        to_core(k).wait_recv()
-        total = keep[k] + drecv[k].astype(jnp.float32)
-        left, right = total[:, :col], total[:, col:]
-        xsend[k] = jnp.where(t == 0, right, left).astype(jnp.bfloat16)
-        to_across(k).start()
-        xkeep[k] = jnp.where(t == 0, left, right)
-
-    def stage_c(k):
-        dest = dests[k]
-        to_across(k).wait_recv()
-        xkeep[k] += xrecv[k].astype(jnp.float32)
-
-        def take(side, device_of):
-            device_of(k).wait_recv()
-            xkeep[k] += zrecv[side, dest].astype(jnp.float32)
-        if k < chips - 1:
-            when((dest > e) & has_down, lambda: take(0, to_up))
-            when((dest < e) & has_up, lambda: take(1, to_down))
-            zsend[k] = xkeep[k].astype(jnp.bfloat16)
-            when(dest > e, lambda: to_up(k).start())
-            when(dest < e, lambda: to_down(k).start())
-        else:
-            when(has_down, lambda: take(0, to_up))
-            when(has_up, lambda: take(1, to_down))
-            out_ref[...] = xkeep[k].astype(jnp.bfloat16)
-
-    for step in range(chips + 2):
+            keep[dest] += shared
+            keep[dest, pl.ds(t * half_rows, half_rows), :] += stream_ref[...]
+
+    def stage_b(dest, last):
+        to_core(dest).wait_recv()
+        for c in range(CHUNKS):
+            total = keep[dest, parts[c]] + drecv[dest, parts[c]].astype(jnp.float32)
+            left, right = total[:, :col], total[:, col:]
+            xkeep[dest, parts[c]] = jnp.where(t == 0, left, right)
+            other = jnp.where(t == 0, right, left)
+            if last:
+                spare[parts[c]] = other
+
+                def add(side, c=c):
+                    other_z(dest, side, c).wait_recv()
+                    spare[parts[c]] += orecv[side, parts[c]].astype(jnp.float32)
+                when(has_down, lambda: add(0))
+                when(has_up, lambda: add(1))
+                xsend[dest, parts[c]] = spare[parts[c]].astype(jnp.bfloat16)
+                to_across(dest, c).start()
+            else:
+                xsend[dest, parts[c]] = other.astype(jnp.bfloat16)
+                when(dest == e + 1, lambda c=c: other_z(dest, 0, c).start())
+                when(dest == e - 1, lambda c=c: other_z(dest, 1, c).start())
+                when(jnp.logical_not(near_dest(dest)), lambda c=c: to_across(dest, c).start())
+
+    def stage_c(dest, last):
+        for c in range(CHUNKS):
+            def swap(c=c):
+                to_across(dest, c).wait_recv()
+                xkeep[dest, parts[c]] += xrecv[dest, parts[c]].astype(jnp.float32)
+
+            def take(side, c=c):
+                along_z(dest, side, c).wait_recv()
+                xkeep[dest, parts[c]] += zrecv[side, dest, parts[c]].astype(jnp.float32)
+            if last:
+                swap()
+                when(has_down, lambda: take(0))
+                when(has_up, lambda: take(1))
+                out_ref[parts[c]] = xkeep[dest, parts[c]].astype(jnp.bfloat16)
+            else:
+                when(jnp.logical_not(near_dest(dest)), swap)
+                when((dest > e) & has_down, lambda: take(0))
+                when((dest < e) & has_up, lambda: take(1))
+                zsend[dest, parts[c]] = xkeep[dest, parts[c]].astype(jnp.bfloat16)
+                when(dest > e, lambda c=c: along_z(dest, 0, c).start())
+                when(dest < e, lambda c=c: along_z(dest, 1, c).start())
+
+    for step in range(chips + 1):
         if step < chips:
-            stage_a(step)
-        if 0 <= step - 1 < chips:
-            stage_b(step - 1)
-        if 0 <= step - 2 < chips:
-            stage_c(step - 2)
+            stage_a(sooner[step], step == chips - 1)
+        if step >= 1:
+            stage_b(sooner[step - 1], step == chips)
     for k in range(chips):
-        to_core(k).wait_send()
-        to_across(k).wait_send()
-        if k < chips - 1:
-            to_up(k).wait_send()
+        stage_c(later[k], k == chips - 1)
+    for k in range(chips):
+        dest = sooner[k]
+        to_core(dest).wait_send()
+        for c in range(CHUNKS):
+            to_across(dest, c).wait_send()
+            if k < chips - 1:
+                along_z(dest, 0, c).wait_send()
 
 
 def gathered(
@@ -446,46 +516,46 @@
     depth = shared_gate_up.shape[0]
     sff = shared_gate_up.shape[2]
     wide = pad_lanes(width)
-    kv_flat = keys_values.reshape(rows, -1)
-    sgu = shared_gate_up.reshape(depth, 2 * sff)
+    kv_flat = keys_values.reshape(-1, keys_values.shape[2])
     vmem = pl.BlockSpec(memory_space=pltpu.VMEM)
     smem = pl.BlockSpec(memory_space=pltpu.SMEM)
     bf16, f32 = jnp.bfloat16, jnp.float32
     dma = pltpu.SemaphoreType.DMA
-    pieces = 4 * chips
+    pieces = 4 * chips * CHUNKS
     nbuf, stream, sgu_full, sdn_full = pl.pallas_call(
         functools.partial(front_kernel, chips),
         name="front",
         out_shape=(
-            jax.ShapeDtypeStruct((chips, 2, 2, rows // 2, wide), bf16),
+            jax.ShapeDtypeStruct((chips, 2, 2, CHUNKS, rows // 2 // CHUNKS, wide), bf16),
             jax.ShapeDtypeStruct((rows // 2, width), f32),
-            jax.ShapeDtypeStruct((2 * depth, 2 * sff), bf16),
-            jax.ShapeDtypeStruct((2, sff, col), bf16),
+            jax.ShapeDtypeStruct((2 * depth, 2, sff), bf16),
+            jax.ShapeDtypeStruct((2, col, sff), bf16),
         ),
-        in_specs=[vmem, vmem, vmem, smem] + [vmem] * 6,
+        in_specs=[vmem, vmem, vmem, smem, vmem, vmem, pl.BlockSpec(memory_space=pltpu.HBM)] + [vmem] * 3,
         out_specs=(vmem,) * 4,
         scratch_shapes=[
             pltpu.VMEM(kv_flat.shape, bf16),
-            pltpu.VMEM((inner, col), bf16),
+            pltpu.VMEM((col, inner), bf16),
             pltpu.VMEM((rows, inner), bf16),
             pltpu.VMEM((rows, width), f32),
             pltpu.VMEM((rows // 2, width), bf16),
             pltpu.VMEM((rows // 2, width), bf16),
-            dma((3,)), dma((3,)), dma((2,)), dma((2,)), dma((4, pieces)), dma((pieces,)),
+            pltpu.VMEM((rows, LANES), f32),
+            dma((3,)), dma((3,)), dma((2,)), dma((2,)), dma, dma((4, pieces)), dma((pieces,)),
         ],
         compiler_params=pltpu.CompilerParams(
             collective_id=0, has_side_effects=True, vmem_limit_bytes=40 * 1024 * 1024
         ),
-    )(queries, kv_flat, residual, sink_logits, norm_gain.reshape(1, -1), out_proj, sgu, shared_down,
-      expert_ids, gate_weights)
+    )(queries, kv_flat, residual.T, sink_logits, norm_gain, out_proj.T, shared_gate_up, shared_down.T,
+      expert_ids.T, gate_weights.T)
     flat = nbuf.reshape(2 * chips * rows, wide)
     tokens = flat[:, :width]
     pre = jnp.einsum("pd,dhf->phf", tokens, expert_gate_up[0], preferred_element_type=f32)
     hidden = glu_act(pre[:, 0], pre[:, 1]).astype(bf16)
     block_index = lax.axis_index(("expert", "seq"))
     here = lax.dynamic_slice_in_dim(flat, block_index * rows, rows, 0)[:, :width]
-    shared_pre = jnp.dot(here, sgu_full, preferred_element_type=f32)
-    shared_hidden = glu_act(shared_pre[:, :sff], shared_pre[:, sff:]).astype(bf16)
+    shared_pre = jnp.einsum("pd,dcf->pcf", here, sgu_full, preferred_element_type=f32)
+    shared_hidden = glu_act(shared_pre[:, 0], shared_pre[:, 1]).astype(bf16)
     edge = width // LANES * LANES
     return pl.pallas_call(
         functools.partial(back_kernel, chips),
@@ -502,7 +572,10 @@
             pltpu.VMEM((chips, rows, col), bf16),
             pltpu.VMEM((chips, rows, col), bf16),
             pltpu.VMEM((2, chips, rows, col), bf16),
-            dma((chips,)), dma((chips,)), dma((chips,)), dma((chips,)), dma((chips,)), dma((2, chips)),
+            pltpu.VMEM((2, rows, col), bf16),
+            pltpu.VMEM((rows, col), f32),
+            dma((chips,)), dma((chips,)), dma((chips, CHUNKS)), dma((chips, CHUNKS)), dma((chips, CHUNKS)),
+            dma((2, chips, CHUNKS)), dma((2, CHUNKS)),
         ],
         compiler_params=pltpu.CompilerParams(
             collective_id=1, has_side_effects=True, vmem_limit_bytes=40 * 1024 * 1024

time: 84.3 us -> 83.8 us (level)
  the two profiles are of different devices: /device:TPU:16 before, /device:TPU:0 now
where the time goes in v2:
time: 83.8 us; the launch traced here: 83.3 us
  Pallas kernels  66.4 us (79%)
  local copies, waits for them, and re-layouts  10.5 us (13%)
  matrix products  5.41 us (6%)
  other arithmetic  0.95 us (1%)
    pallas_call x1, Pallas kernels, gathered(): pl.pallas_call(functools.partial(front_kernel, chips), name='front', out_...  40.7 us
    pallas_call x1, Pallas kernels, gathered(): pl.pallas_call(functools.partial(back_kernel, chips), name='back', out_sh...  25.6 us
    unnamed x24, local copies, waits for them, and re-layouts  9.68 us
    dot_general x1, matrix products, gathered(): jnp.einsum('pd,dhf->phf', tokens, expert_gate_up[0], preferred_element_ty...  5.03 us

profile of v2, /device:TPU:0, one launch (start us, length us, event | category | flops | bytes accessed | tf_op | source)
XLA Modules:
  0.0 83.3 jit_solution(1139674366401958956)
XLA Ops:
  0.0 0.0 copy-start.1
  0.0 1.4 %copy-done.1 = bf16[1024,720]{0,1:T(8,128)(2,1)S(1)} copy-done((bf16[1024,720]{0,1:T(8,128)(2,1)S(1)}, bf16[1024,720]{0,1:T(8,128)(2,1)}, u32[]{:S(2)}) %copy-start.1) | copy-done | bytes 1474584
  1.4 0.0 copy-start.2
  1.4 1.1 %copy-done.2 = bf16[720,2,256]{2,1,0:T(2,128)(2,1)S(1)} copy-done((bf16[720,2,256]{2,1,0:T(2,128)(2,1)S(1)}, bf16[720,2,256]{2,1,0:T(2,128)(2,1)}, u32[]{:S(2)}) %copy-start.2) | copy-done | bytes 737304
  2.5 0.0 copy-start.3
  2.5 1.0 %copy-done.3 = bf16[128,1440]{0,1:T(8,128)(2,1)S(1)} copy-done((bf16[128,1440]{0,1:T(8,128)(2,1)S(1)}, bf16[128,1440]{0,1:T(8,128)(2,1)}, u32[]{:S(2)}) %copy-start.3) | copy-done | bytes 368664
  3.5 0.0 copy-start.4
  3.5 1.0 %copy-done.4 = bf16[256,720]{0,1:T(8,128)(2,1)S(1)} copy-done((bf16[256,720]{0,1:T(8,128)(2,1)S(1)}, bf16[256,720]{0,1:T(8,128)(2,1)}, u32[]{:S(2)}) %copy-start.4) | copy-done | bytes 368664
  4.5 0.0 copy-start.5
  4.5 0.9 %copy-done.5 = bf16[128,1024]{1,0:T(8,128)(2,1)S(1)} copy-done((bf16[128,1024]{1,0:T(8,128)(2,1)S(1)}, bf16[128,1024]{1,0:T(8,128)(2,1)}, u32[]{:S(2)}) %copy-start.5) | copy-done | bytes 262168
  5.4 0.0 copy-start.6
  5.4 0.8 %copy-done.6 = bf16[128,2,128]{2,1,0:T(2,128)(2,1)S(1)} copy-done((bf16[128,2,128]{2,1,0:T(2,128)(2,1)S(1)}, bf16[128,2,128]{2,1,0:T(2,128)(2,1)}, u32[]{:S(2)}) %copy-start.6) | copy-done | bytes 65560
  6.3 0.0 copy-start.7
  6.3 0.7 copy-done.7
  7.0 0.0 copy-start.8
  7.0 0.7 copy-done.8
  7.6 0.0 copy-start.9
  7.6 0.7 copy-done.9
  8.3 0.0 copy-start.10
  8.3 0.7 copy-done.10
  9.0 0.0 copy-start.11
  9.0 40.7 %front.1 = (bf16[4,2,2,2,32,1536]{5,4,3,2,1,0:T(8,128)(2,1)S(1)}, f32[64,1440]{1,0:T(8,128)S(1)}, bf16[1440,2,256]{2,1,0:T(2,128)(2,1)S(1)}, bf16[2,720,256]{2,1,0:T(8,128)(2,1)S(1)}) custom-call(bf16[128,1024]{1,0:T(8,128)(2,1)S(1)} %copy-done.5, bf16[256,128]{1,0:T(8,128)(2,1)S(1)} %bitcast.23, bf16[1440,128]{1,0:T(8,128)(2,1)S(1)} %bitcast.21, ...), custom_call_target="tpu_custom_call" | custom-call | tf_op jit(solution)/shard_map/front/pallas_call | solution.py:525
  49.7 0.4 fusion.6
  50.2 0.0 copy-done.11
  50.2 5.0 %fusion = f32[1024,2,720]{2,0,1:T(8,128)S(1)} fusion(bf16[1440,2,720]{2,1,0:T(2,128)(2,1)S(1)} %bitcast.29, bf16[1024,1536]{1,0:T(8,128)(2,1)S(1)} %bitcast.26), kind=kOutput, calls=%fused_computation | convolution fusion | flops 4246732800 | bytes 13191168 | tf_op jit(solution)/shard_map/pd,dhf->phf/dot_general | solution.py:553
  55.2 0.0 copy-start
  55.3 0.9 %fusion.5.hidden_ref = bf16[1024,720]{1,0:T(8,128)(2,1)S(1)} fusion(f32[1024,2,720]{2,0,1:T(8,128)S(1)} %fusion), kind=kLoop, calls=%fused_computation.7 | loop fusion | flops 5898240 | bytes 7372800 | tf_op jit(solution)/shard_map/convert_element_type | solution.py:554
  56.2 0.7 copy-done
  56.9 25.6 %back.1 = bf16[128,720]{1,0:T(8,128)(2,1)S(1)} custom-call(bf16[1024,720]{1,0:T(8,128)(2,1)S(1)} %fusion.5.hidden_ref, bf16[720,1440]{1,0:T(8,128)(2,1)S(1)} %bitcast.19, bf16[1024,128]{1,0:T(8,128)(2,1)S(1)} %slice.31.gate_ref, bf16[128,256]{1,0:T(8,128)(2,1)S(1)} %fusion.11.sh_ref, bf16[2,720,256]{2,1,0:T(8,128)(2,1)S(1)} %get-tuple-element.11.sdn_ref, ...), custom_call_target="tpu_custom_call" | custom-call | tf_op jit(solution)/shard_map/back/pallas_call | solution.py:560
  82.5 0.8 copy.19
  (2 shorter events, 0.1 us)
Async XLA Ops:
  0.0 1.4 %copy-start.1 = (bf16[1024,720]{0,1:T(8,128)(2,1)S(1)}, bf16[1024,720]{0,1:T(8,128)(2,1)}, u32[]{:S(2)}) copy-start(bf16[1024,720]{0,1:T(8,128)(2,1)} %param.17) | copy-start | bytes 4423684
  1.4 1.1 %copy-start.2 = (bf16[720,2,256]{2,1,0:T(2,128)(2,1)S(1)}, bf16[720,2,256]{2,1,0:T(2,128)(2,1)}, u32[]{:S(2)}) copy-start(bf16[720,2,256]{2,1,0:T(2,128)(2,1)} %sgu_ref.1) | copy-start | bytes 2211844
  2.5 1.0 %copy-start.3 = (bf16[128,1440]{0,1:T(8,128)(2,1)S(1)}, bf16[128,1440]{0,1:T(8,128)(2,1)}, u32[]{:S(2)}) copy-start(bf16[128,1440]{0,1:T(8,128)(2,1)} %param.14) | copy-start | bytes 1105924
  3.5 1.0 %copy-start.4 = (bf16[256,720]{0,1:T(8,128)(2,1)S(1)}, bf16[256,720]{0,1:T(8,128)(2,1)}, u32[]{:S(2)}) copy-start(bf16[256,720]{0,1:T(8,128)(2,1)} %param.19) | copy-start | bytes 1105924
  4.5 0.9 %copy-start.5 = (bf16[128,1024]{1,0:T(8,128)(2,1)S(1)}, bf16[128,1024]{1,0:T(8,128)(2,1)}, u32[]{:S(2)}) copy-start(bf16[128,1024]{1,0:T(8,128)(2,1)} %q_ref.1) | copy-start | bytes 786436
  5.4 0.8 %copy-start.6 = (bf16[128,2,128]{2,1,0:T(2,128)(2,1)S(1)}, bf16[128,2,128]{2,1,0:T(2,128)(2,1)}, u32[]{:S(2)}) copy-start(bf16[128,2,128]{2,1,0:T(2,128)(2,1)} %param.13) | copy-start | bytes 196612
  6.3 0.7 copy-start.7
  7.0 0.7 copy-start.8
  7.6 0.7 copy-start.9
  8.3 0.7 copy-start.10
  9.0 41.2 %copy-start.11 = (bf16[1,1440,2,720]{3,2,1,0:T(2,128)(2,1)S(1)}, bf16[1,1440,2,720]{3,2,1,0:T(2,128)(2,1)}, u32[]{:S(2)}) copy-start(bf16[1,1440,2,720]{3,2,1,0:T(2,128)(2,1)} %param.20) | copy-start | bytes 12441604
  55.2 1.6 %copy-start = (bf16[1,720,1440]{2,1,0:T(8,128)(2,1)S(1)}, bf16[1,720,1440]{2,1,0:T(8,128)(2,1)}, u32[]{:S(2)}) copy-start(bf16[1,720,1440]{2,1,0:T(8,128)(2,1)} %param.21) | copy-start | bytes 6220804

commit v3 on v2

--- a/solution.py
+++ b/solution.py
@@ -136,7 +136,7 @@
 
 MESH_ID = pl.DeviceIdType.MESH
 LANES = 128
-CHUNKS = 2
+CHUNKS = 4
 
 
 def pad_lanes(count):

time: 83.8 us -> 83.4 us (level)
  no operation moved by 1% of the time
where the time goes in v3:
time: 83.4 us; the launch traced here: 83 us
  Pallas kernels  66 us (79%)
  local copies, waits for them, and re-layouts  10.5 us (13%)
  matrix products  5.42 us (6%)
  other arithmetic  0.95 us (1%)
    pallas_call x1, Pallas kernels, gathered(): pl.pallas_call(functools.partial(front_kernel, chips), name='front', out_...  40.3 us
    pallas_call x1, Pallas kernels, gathered(): pl.pallas_call(functools.partial(back_kernel, chips), name='back', out_sh...  25.7 us
    unnamed x24, local copies, waits for them, and re-layouts  9.68 us
    dot_general x1, matrix products, gathered(): jnp.einsum('pd,dhf->phf', tokens, expert_gate_up[0], preferred_element_ty...  5.03 us

profile of v3, /device:TPU:0, one launch (start us, length us, event | category | flops | bytes accessed | tf_op | source)
XLA Modules:
  0.0 83.0 jit_solution(5458714857827645434)
XLA Ops:
  0.0 0.0 copy-start.1
  0.0 1.4 %copy-done.1 = bf16[1024,720]{0,1:T(8,128)(2,1)S(1)} copy-done((bf16[1024,720]{0,1:T(8,128)(2,1)S(1)}, bf16[1024,720]{0,1:T(8,128)(2,1)}, u32[]{:S(2)}) %copy-start.1) | copy-done | bytes 1474584
  1.4 0.0 copy-start.2
  1.4 1.1 %copy-done.2 = bf16[720,2,256]{2,1,0:T(2,128)(2,1)S(1)} copy-done((bf16[720,2,256]{2,1,0:T(2,128)(2,1)S(1)}, bf16[720,2,256]{2,1,0:T(2,128)(2,1)}, u32[]{:S(2)}) %copy-start.2) | copy-done | bytes 737304
  2.5 0.0 copy-start.3
  2.5 1.0 %copy-done.3 = bf16[128,1440]{0,1:T(8,128)(2,1)S(1)} copy-done((bf16[128,1440]{0,1:T(8,128)(2,1)S(1)}, bf16[128,1440]{0,1:T(8,128)(2,1)}, u32[]{:S(2)}) %copy-start.3) | copy-done | bytes 368664
  3.5 0.0 copy-start.4
  3.5 1.0 %copy-done.4 = bf16[256,720]{0,1:T(8,128)(2,1)S(1)} copy-done((bf16[256,720]{0,1:T(8,128)(2,1)S(1)}, bf16[256,720]{0,1:T(8,128)(2,1)}, u32[]{:S(2)}) %copy-start.4) | copy-done | bytes 368664
  4.5 0.0 copy-start.5
  4.5 0.9 %copy-done.5 = bf16[128,1024]{1,0:T(8,128)(2,1)S(1)} copy-done((bf16[128,1024]{1,0:T(8,128)(2,1)S(1)}, bf16[128,1024]{1,0:T(8,128)(2,1)}, u32[]{:S(2)}) %copy-start.5) | copy-done | bytes 262168
  5.4 0.0 copy-start.6
  5.4 0.8 %copy-done.6 = bf16[128,2,128]{2,1,0:T(2,128)(2,1)S(1)} copy-done((bf16[128,2,128]{2,1,0:T(2,128)(2,1)S(1)}, bf16[128,2,128]{2,1,0:T(2,128)(2,1)}, u32[]{:S(2)}) %copy-start.6) | copy-done | bytes 65560
  6.3 0.0 copy-start.7
  6.3 0.7 copy-done.7
  7.0 0.0 copy-start.8
  7.0 0.7 copy-done.8
  7.6 0.0 copy-start.9
  7.6 0.7 copy-done.9
  8.3 0.0 copy-start.10
  8.3 0.7 copy-done.10
  9.0 0.0 copy-start.11
  9.0 40.3 %front.1 = (bf16[4,2,2,4,16,1536]{5,4,3,2,1,0:T(8,128)(2,1)S(1)}, f32[64,1440]{1,0:T(8,128)S(1)}, bf16[1440,2,256]{2,1,0:T(2,128)(2,1)S(1)}, bf16[2,720,256]{2,1,0:T(8,128)(2,1)S(1)}) custom-call(bf16[128,1024]{1,0:T(8,128)(2,1)S(1)} %copy-done.5, bf16[256,128]{1,0:T(8,128)(2,1)S(1)} %bitcast.23, bf16[1440,128]{1,0:T(8,128)(2,1)S(1)} %bitcast.21, ...), custom_call_target="tpu_custom_call" | custom-call | tf_op jit(solution)/shard_map/front/pallas_call | solution.py:525
  49.3 0.4 fusion.6
  49.8 0.0 copy-done.11
  49.8 5.0 %fusion = f32[1024,2,720]{2,0,1:T(8,128)S(1)} fusion(bf16[1440,2,720]{2,1,0:T(2,128)(2,1)S(1)} %bitcast.29, bf16[1024,1536]{1,0:T(8,128)(2,1)S(1)} %bitcast.26), kind=kOutput, calls=%fused_computation | convolution fusion | flops 4246732800 | bytes 13191168 | tf_op jit(solution)/shard_map/pd,dhf->phf/dot_general | solution.py:553
  54.8 0.0 copy-start
  54.8 0.9 %fusion.5.hidden_ref = bf16[1024,720]{1,0:T(8,128)(2,1)S(1)} fusion(f32[1024,2,720]{2,0,1:T(8,128)S(1)} %fusion), kind=kLoop, calls=%fused_computation.7 | loop fusion | flops 5898240 | bytes 7372800 | tf_op jit(solution)/shard_map/convert_element_type | solution.py:554
  55.7 0.7 copy-done
  56.4 25.7 %back.1 = bf16[128,720]{1,0:T(8,128)(2,1)S(1)} custom-call(bf16[1024,720]{1,0:T(8,128)(2,1)S(1)} %fusion.5.hidden_ref, bf16[720,1440]{1,0:T(8,128)(2,1)S(1)} %bitcast.19, bf16[1024,128]{1,0:T(8,128)(2,1)S(1)} %slice.31.gate_ref, bf16[128,256]{1,0:T(8,128)(2,1)S(1)} %fusion.11.sh_ref, bf16[2,720,256]{2,1,0:T(8,128)(2,1)S(1)} %get-tuple-element.11.sdn_ref, ...), custom_call_target="tpu_custom_call" | custom-call | tf_op jit(solution)/shard_map/back/pallas_call | solution.py:560
  82.2 0.8 copy.19
  (2 shorter events, 0.1 us)
Async XLA Ops:
  0.0 1.4 %copy-start.1 = (bf16[1024,720]{0,1:T(8,128)(2,1)S(1)}, bf16[1024,720]{0,1:T(8,128)(2,1)}, u32[]{:S(2)}) copy-start(bf16[1024,720]{0,1:T(8,128)(2,1)} %param.17) | copy-start | bytes 4423684
  1.4 1.1 %copy-start.2 = (bf16[720,2,256]{2,1,0:T(2,128)(2,1)S(1)}, bf16[720,2,256]{2,1,0:T(2,128)(2,1)}, u32[]{:S(2)}) copy-start(bf16[720,2,256]{2,1,0:T(2,128)(2,1)} %sgu_ref.1) | copy-start | bytes 2211844
  2.5 1.0 %copy-start.3 = (bf16[128,1440]{0,1:T(8,128)(2,1)S(1)}, bf16[128,1440]{0,1:T(8,128)(2,1)}, u32[]{:S(2)}) copy-start(bf16[128,1440]{0,1:T(8,128)(2,1)} %param.14) | copy-start | bytes 1105924
  3.5 1.0 %copy-start.4 = (bf16[256,720]{0,1:T(8,128)(2,1)S(1)}, bf16[256,720]{0,1:T(8,128)(2,1)}, u32[]{:S(2)}) copy-start(bf16[256,720]{0,1:T(8,128)(2,1)} %param.19) | copy-start | bytes 1105924
  4.5 0.9 %copy-start.5 = (bf16[128,1024]{1,0:T(8,128)(2,1)S(1)}, bf16[128,1024]{1,0:T(8,128)(2,1)}, u32[]{:S(2)}) copy-start(bf16[128,1024]{1,0:T(8,128)(2,1)} %q_ref.1) | copy-start | bytes 786436
  5.4 0.8 %copy-start.6 = (bf16[128,2,128]{2,1,0:T(2,128)(2,1)S(1)}, bf16[128,2,128]{2,1,0:T(2,128)(2,1)}, u32[]{:S(2)}) copy-start(bf16[128,2,128]{2,1,0:T(2,128)(2,1)} %param.13) | copy-start | bytes 196612
  6.3 0.7 copy-start.7
  7.0 0.7 copy-start.8
  7.6 0.7 copy-start.9
  8.3 0.7 copy-start.10
  9.0 40.8 %copy-start.11 = (bf16[1,1440,2,720]{3,2,1,0:T(2,128)(2,1)S(1)}, bf16[1,1440,2,720]{3,2,1,0:T(2,128)(2,1)}, u32[]{:S(2)}) copy-start(bf16[1,1440,2,720]{3,2,1,0:T(2,128)(2,1)} %param.20) | copy-start | bytes 12441604
  54.8 1.6 %copy-start = (bf16[1,720,1440]{2,1,0:T(8,128)(2,1)S(1)}, bf16[1,720,1440]{2,1,0:T(8,128)(2,1)}, u32[]{:S(2)}) copy-start(bf16[1,720,1440]{2,1,0:T(8,128)(2,1)} %param.21) | copy-start | bytes 6220804
